TPU v7x, 32 devices: a whole 2x2x4 slice. The times are simulated.
32 devices in a mesh: row: 4 (over z), col: 8 (over y, x, core).
Axes of the slice: x: 2, y: 2, z: 4, core: 2. Of those that a mesh axis runs over, the one named last changes fastest.
Arguments:
- neighbor: int32 [32, 3072, 3072], P(None, 'col', 'row'), may hold values from 0 to 1, as said below
- true_coords: float32 [32, 3, 3072], P(None, None, ('row', 'col')), as said below
- pred_coords: float32 [32, 3, 3072], P(None, None, ('row', 'col')), as said below
- residue_mask: int32 [32, 3072], P(None, ('row', 'col')), may hold values from 0 to 1, as said below
- single: bfloat16 [32, 3072, 384], P(None, ('row', 'col'))
- ln_gain: float32 [384], replicated, may hold values from 0.1 to 1.9
- w_hidden: bfloat16 [384, 128], replicated, may hold values from -0.3125 to 0.3125
- b_hidden: float32 [128], replicated, may hold values from -3 to 3
- w_mid: bfloat16 [128, 128], replicated, may hold values from -0.5 to 0.5
- b_mid: float32 [128], replicated, may hold values from -3 to 3
- w_logits: bfloat16 [128, 50], replicated, may hold values from -1.5 to 1.5
- b_logits: float32 [50], replicated, may hold values from -4 to 4
Outputs:
- lddt_score: float32 [32, 3072], P(None, ('row', 'col'))
- residue_loss: float32 [32, 3072], P(None, ('row', 'col'))
- total_loss: float32 [], replicated
Inputs may be any that keep to these rules, and one draw needn't show every extreme that they name: `neighbor`: 0 or 1; 0 where j == i; 1 wherever 0 < |i - j| <= 8. `residue_mask`: per structure, 1 on a leading run of 1536 or more residues and 0 after it. `true_coords`: positions in angstroms. `pred_coords`: positions in angstroms.
All inputs are finite; a program needn't handle non-finite values.
Results may differ from a plain program's by a relative error of at most 0.00098.
Values sent between devices are 32-bit elements; how exact they have to be, the bound alone decides.
A program may use at most 128 MiB of HBM per device.

v0:
```python
import functools

import jax
import jax.numpy as jnp
from jax import lax
from jax.experimental import pallas as pl
from jax.experimental.pallas import tpu as pltpu
from jax.sharding import PartitionSpec as P

THRESHOLDS = (0.5, 1.0, 2.0, 4.0)
EPS = 1e-10
MESH = pl.DeviceIdType.MESH


def gather_kernel(R, C, x_ref, rows_ref, cols_ref, send_sem, recv_sem, csend_sem, crecv_sem):
    r = lax.axis_index("row")
    c = lax.axis_index("col")
    g = r * C + c
    to_col = g // R
    slot = g % R
    own = to_col == c

    barrier = pltpu.get_barrier_semaphore()
    for k in range(1, C):
        pl.semaphore_signal(barrier, inc=1, device_id=(r, (c + k) % C), device_id_type=MESH)
    for s in range(R):
        source = R * c + s

        @pl.when(source != g)
        def _():
            pl.semaphore_signal(barrier, inc=1, device_id=(source // C, source % C), device_id_type=MESH)

    pl.semaphore_wait(barrier, C - 1 + R - jnp.where(own, 1, 0))

    col_copies = []
    for k in range(1, R):
        copy = pltpu.make_async_remote_copy(
            src_ref=x_ref,
            dst_ref=cols_ref.at[slot],
            send_sem=csend_sem.at[k],
            recv_sem=crecv_sem.at[slot],
            device_id=((r + k) % R, to_col),
            device_id_type=MESH,
        )
        copy.start()
        col_copies.append(copy)
    home = pltpu.make_async_remote_copy(
        src_ref=x_ref,
        dst_ref=cols_ref.at[slot],
        send_sem=csend_sem.at[0],
        recv_sem=crecv_sem.at[slot],
        device_id=(r, to_col),
        device_id_type=MESH,
    )

    @pl.when(jnp.logical_not(own))
    def _():
        home.start()

    row_copies = []
    for k in range(1, C):
        copy = pltpu.make_async_remote_copy(
            src_ref=x_ref,
            dst_ref=rows_ref.at[c],
            send_sem=send_sem.at[k],
            recv_sem=recv_sem.at[k],
            device_id=(r, (c + k) % C),
            device_id_type=MESH,
        )
        copy.start()
        row_copies.append(copy)

    rows_ref[c] = x_ref[...]

    @pl.when(own)
    def _():
        cols_ref[slot] = x_ref[...]

    for copy in row_copies:
        copy.wait()
    for copy in col_copies:
        copy.wait_send()

    @pl.when(jnp.logical_not(own))
    def _():
        home.wait_send()

    for s in range(R):

        @pl.when(R * c + s != g)
        def _():
            pltpu.make_async_remote_copy(
                src_ref=x_ref,
                dst_ref=cols_ref.at[s],
                send_sem=csend_sem.at[0],
                recv_sem=crecv_sem.at[s],
                device_id=(r, to_col),
                device_id_type=MESH,
            ).wait_recv()


def gather(x, R, C):
    shape = x.shape
    return pl.pallas_call(
        functools.partial(gather_kernel, R, C),
        out_shape=(
            jax.ShapeDtypeStruct((C,) + shape, x.dtype),
            jax.ShapeDtypeStruct((R,) + shape, x.dtype),
        ),
        in_specs=[pl.BlockSpec(memory_space=pltpu.VMEM)],
        out_specs=[pl.BlockSpec(memory_space=pltpu.VMEM)] * 2,
        scratch_shapes=[
            pltpu.SemaphoreType.DMA((C,)),
            pltpu.SemaphoreType.DMA((C,)),
            pltpu.SemaphoreType.DMA((R,)),
            pltpu.SemaphoreType.DMA((R,)),
        ],
        compiler_params=pltpu.CompilerParams(collective_id=0, has_side_effects=True),
        name="gather",
    )(x)


def split3(x):
    first = x.astype(jnp.bfloat16).astype(jnp.float32)
    rest = x - first
    second = rest.astype(jnp.bfloat16).astype(jnp.float32)
    return first, second, rest - second


def with_norms(x, row):
    square = x * x
    true_norm = square[0:1] + square[1:2] + square[2:3]
    pred_norm = square[3:4] + square[4:5] + square[5:6]
    mixed = jnp.where(row < 6, x, jnp.where(row == 6, true_norm, pred_norm))
    return mixed, true_norm, pred_norm


def pair_kernel(
    R, C, chunk,
    rows_ref, cols_ref, neighbor_ref, single_ref, gain_ref, wh_ref, bh_ref, wm_ref, bm_ref, wl_ref, bl_ref,
    parts_ref, logits_ref, total_ref,
    left_t, left_p, right, d_true, d_pred, acc_p, acc_n,
):
    b = pl.program_id(0)
    batch = pl.num_programs(0)
    own_len = rows_ref.shape[3]
    rows_len = C * own_len
    cols_len = R * own_len
    rows = jnp.concatenate([rows_ref[s, b] for s in range(C)], axis=1)
    cols = jnp.concatenate([cols_ref[s, b] for s in range(R)], axis=1)
    keep = cols[6:7]
    center = jnp.sum(cols * keep, axis=1, keepdims=True) / jnp.maximum(jnp.sum(keep, axis=1, keepdims=True), 1.0)
    row_r = lax.broadcasted_iota(jnp.int32, rows.shape, 0)
    row_c = lax.broadcasted_iota(jnp.int32, cols.shape, 0)
    far, _, _ = with_norms((rows - center) * 2.0, row_r)
    near = (cols - center) * 2.0
    _, near_t, near_p = with_norms(near, row_c)
    f1, f2, f3 = split3(far)
    ones = jnp.ones_like(far)
    right[...] = jnp.concatenate([f1, f1, f1, f2, f2, f3, ones, jnp.zeros_like(far)], axis=0).astype(jnp.bfloat16)
    n1, n2, n3 = split3(near)
    zeros = jnp.zeros_like(near)
    for ref, low, norm_row, norm in ((left_t, 0, 6, near_t), (left_p, 3, 7, near_p)):
        inside = (row_c >= low) & (row_c < low + 3)
        l1 = jnp.where(inside, -2.0 * n1, jnp.where(row_c == norm_row, 1.0, 0.0))
        l2 = jnp.where(inside, -2.0 * n2, 0.0)
        l3 = jnp.where(inside, -2.0 * n3, 0.0)
        m1, m2, m3 = split3(norm)
        tail = jnp.where(
            row_c == 0, m1, jnp.where(row_c == 1, m2, jnp.where(row_c == 2, m3, jnp.where(row_c == 3, 4.0 * EPS, 0.0)))
        )
        side = jnp.concatenate([l1, l2, l3, l1, l2, l1, tail, zeros], axis=0)
        ref[...] = jnp.transpose(side).astype(jnp.bfloat16)
    keep_col = jnp.transpose(cols)[:, 6:7]
    width = 256
    step = 16
    for q in range(rows_len // width):
        lanes = slice(q * width, (q + 1) * width)
        half = q % 2
        weights_side = right[:, lanes]
        d_true[half] = jnp.dot(left_t[...], weights_side, preferred_element_type=jnp.float32)
        d_pred[half] = jnp.dot(left_p[...], weights_side, preferred_element_type=jnp.float32)
        total_p = jnp.zeros((8, width), jnp.float32)
        total_n = jnp.zeros((8, width), jnp.float32)
        for j in range(0, cols_len, step):
            span = slice(j, j + step)
            t2 = jnp.maximum(d_true[half, span, :], 4.0 * EPS)
            p2 = jnp.maximum(d_pred[half, span, :], 4.0 * EPS)
            gap = jnp.abs(p2 * lax.rsqrt(p2) - t2 * lax.rsqrt(t2))
            w = neighbor_ref[0, span, lanes].astype(jnp.float32) * keep_col[span]
            score = jnp.tanh(2.0 * THRESHOLDS[0] - gap)
            for threshold in THRESHOLDS[1:]:
                score = score + jnp.tanh(2.0 * threshold - gap)
            score = score * w
            for h in range(0, step, 8):
                total_p = total_p + score[h : h + 8]
                total_n = total_n + w[h : h + 8]
        count = jnp.sum(total_n, axis=0, keepdims=True)
        acc_n[pl.ds(b, 1), lanes] = count
        acc_p[pl.ds(b, 1), lanes] = 0.5 * count + 0.125 * jnp.sum(total_p, axis=0, keepdims=True)

    features = single_ref[0].astype(jnp.float32)
    average = jnp.mean(features, axis=-1, keepdims=True)
    centred = features - average
    variance = jnp.mean(centred * centred, axis=-1, keepdims=True)
    normed = (centred * lax.rsqrt(variance + 1e-05) * gain_ref[...]).astype(jnp.bfloat16)
    first = jnp.maximum(
        jnp.dot(normed, wh_ref[...], preferred_element_type=jnp.float32) + bh_ref[...], 0.0
    ).astype(jnp.bfloat16)
    second = jnp.maximum(
        jnp.dot(first, wm_ref[...], preferred_element_type=jnp.float32) + bm_ref[...], 0.0
    ).astype(jnp.bfloat16)
    logits = (
        lax.dot_general(wl_ref[...], second, (((1,), (1,)), ((), ())), preferred_element_type=jnp.float32)
        + bl_ref[...]
    )
    logits_ref[0] = logits
    total_ref[pl.ds(b, 1), :] = jnp.log(jnp.sum(jnp.exp(logits), axis=0, keepdims=True))

    @pl.when(b == batch - 1)
    def _():
        count = acc_p.shape[0]
        for s in range(C):
            lanes = slice(s * own_len, (s + 1) * own_len)
            parts_ref[s, 0:count, :] = acc_p[:, lanes]
            parts_ref[s, count:, :] = acc_n[:, lanes]


def pairs(rows, cols, neighbor, single, gain, wh, bh, wm, bm, wl, bl, R, C):
    batch, cols_len, rows_len = neighbor.shape
    own_len = rows.shape[3]
    bins = wl.shape[0]
    whole = pl.BlockSpec(memory_space=pltpu.VMEM)
    return pl.pallas_call(
        functools.partial(pair_kernel, R, C, 16),
        grid=(batch,),
        in_specs=[
            whole,
            whole,
            pl.BlockSpec((1, cols_len, rows_len), lambda i: (i, 0, 0)),
            pl.BlockSpec((1,) + single.shape[1:], lambda i: (i, 0, 0)),
        ]
        + [whole] * 7,
        out_specs=[
            pl.BlockSpec((C, 2 * batch, own_len), lambda i: (0, 0, 0)),
            pl.BlockSpec((1, bins, own_len), lambda i: (i, 0, 0)),
            pl.BlockSpec((batch, own_len), lambda i: (0, 0)),
        ],
        out_shape=[
            jax.ShapeDtypeStruct((C, 2 * batch, own_len), jnp.float32),
            jax.ShapeDtypeStruct((batch, bins, own_len), jnp.float32),
            jax.ShapeDtypeStruct((batch, own_len), jnp.float32),
        ],
        scratch_shapes=[
            pltpu.VMEM((cols_len, 64), jnp.bfloat16),
            pltpu.VMEM((cols_len, 64), jnp.bfloat16),
            pltpu.VMEM((64, rows_len), jnp.bfloat16),
            pltpu.VMEM((2, cols_len, 256), jnp.float32),
            pltpu.VMEM((2, cols_len, 256), jnp.float32),
            pltpu.VMEM((batch, rows_len), jnp.float32),
            pltpu.VMEM((batch, rows_len), jnp.float32),
        ],
        compiler_params=pltpu.CompilerParams(dimension_semantics=("arbitrary",)),
        name="pairs",
    )(rows, cols, neighbor, single, gain, wh, bh, wm, bm, wl, bl)


def finish_kernel(
    R, C,
    parts_ref, logits_ref, total_ref, valid_ref,
    lddt_ref, loss_ref, mean_ref,
    landed, tile, mid, tiles_c, tiles_r,
    send_sem, recv_sem, csend_sem, crecv_sem, rsend_sem, rrecv_sem,
):
    r = lax.axis_index("row")
    c = lax.axis_index("col")
    barrier = pltpu.get_barrier_semaphore()
    for k in range(1, C):
        pl.semaphore_signal(barrier, inc=1, device_id=(r, (c + k) % C), device_id_type=MESH)
    for k in range(1, R):
        pl.semaphore_signal(barrier, inc=1, device_id=((r + k) % R, c), device_id_type=MESH)
    pl.semaphore_wait(barrier, C + R - 2)

    copies = []
    for k in range(1, C):
        peer = (c + k) % C
        copy = pltpu.make_async_remote_copy(
            src_ref=parts_ref.at[peer],
            dst_ref=landed.at[k],
            send_sem=send_sem.at[k],
            recv_sem=recv_sem.at[k],
            device_id=(r, peer),
            device_id_type=MESH,
        )
        copy.start()
        copies.append(copy)
    sums = parts_ref[c]
    for copy in copies:
        copy.wait()
    for k in range(1, C):
        sums = sums + landed[k]
    batch = valid_ref.shape[0]
    valid = valid_ref[...]
    lddt = valid * sums[0:batch] / jnp.maximum(valid * sums[batch:], 1.0)
    lddt_ref[...] = lddt
    bins = logits_ref.shape[1]
    logits = logits_ref[...]
    centers = (lax.broadcasted_iota(jnp.int32, logits.shape, 1).astype(jnp.float32) + 0.5) / bins
    apart = lddt[:, None, :] - centers
    closeness = jnp.exp(-(apart * apart) * (bins * bins * 0.5))
    expected = jnp.sum(closeness * logits, axis=1) / jnp.sum(closeness, axis=1)
    loss = valid * (total_ref[...] - expected)
    own_len = valid.shape[1]
    tile[...] = jnp.zeros_like(tile)
    tile[0:1, 0:own_len] = jnp.sum(loss, axis=0, keepdims=True)
    tile[1:2, 0:own_len] = jnp.sum(valid, axis=0, keepdims=True)
    loss_ref[...] = loss

    copies = []
    for k in range(1, C):
        copy = pltpu.make_async_remote_copy(
            src_ref=tile,
            dst_ref=tiles_c.at[c],
            send_sem=csend_sem.at[k],
            recv_sem=crecv_sem.at[k],
            device_id=(r, (c + k) % C),
            device_id_type=MESH,
        )
        copy.start()
        copies.append(copy)
    for copy in copies:
        copy.wait()
    tiles_c[c] = tile[...]
    summed = tiles_c[0]
    for k in range(1, C):
        summed = summed + tiles_c[k]
    mid[...] = summed
    copies = []
    for k in range(1, R):
        copy = pltpu.make_async_remote_copy(
            src_ref=mid,
            dst_ref=tiles_r.at[r],
            send_sem=rsend_sem.at[k],
            recv_sem=rrecv_sem.at[k],
            device_id=((r + k) % R, c),
            device_id_type=MESH,
        )
        copy.start()
        copies.append(copy)
    for copy in copies:
        copy.wait()
    tiles_r[r] = mid[...]
    final = tiles_r[0]
    for k in range(1, R):
        final = final + tiles_r[k]
    both = jnp.sum(final, axis=1, keepdims=True)
    mean_ref[...] = jnp.broadcast_to(both[0:1] / both[1:2], mean_ref.shape)


def finish(parts, logits, total, valid, R, C):
    own = valid.shape
    vmem = pl.BlockSpec(memory_space=pltpu.VMEM)
    return pl.pallas_call(
        functools.partial(finish_kernel, R, C),
        out_shape=(
            jax.ShapeDtypeStruct(own, jnp.float32),
            jax.ShapeDtypeStruct(own, jnp.float32),
            jax.ShapeDtypeStruct((8, 128), jnp.float32),
        ),
        in_specs=[vmem] * 4,
        out_specs=[vmem] * 3,
        scratch_shapes=[
            pltpu.VMEM(parts.shape, jnp.float32),
            pltpu.VMEM((8, 128), jnp.float32),
            pltpu.VMEM((8, 128), jnp.float32),
            pltpu.VMEM((C, 8, 128), jnp.float32),
            pltpu.VMEM((R, 8, 128), jnp.float32),
            pltpu.SemaphoreType.DMA((C,)),
            pltpu.SemaphoreType.DMA((C,)),
            pltpu.SemaphoreType.DMA((C,)),
            pltpu.SemaphoreType.DMA((C,)),
            pltpu.SemaphoreType.DMA((R,)),
            pltpu.SemaphoreType.DMA((R,)),
        ],
        compiler_params=pltpu.CompilerParams(collective_id=1, has_side_effects=True),
        name="finish",
    )(parts, logits, total, valid)


def local(
    R, C,
    neighbor,
    true_coords,
    pred_coords,
    residue_mask,
    single,
    ln_gain,
    w_hidden,
    b_hidden,
    w_mid,
    b_mid,
    w_logits,
    b_logits,
):
    valid = residue_mask.astype(jnp.float32)
    stacked = jnp.concatenate(
        [true_coords, pred_coords, valid[:, None, :], jnp.zeros_like(valid)[:, None, :]], axis=1
    )
    rows, cols = gather(stacked, R, C)
    parts, logits, total = pairs(
        rows,
        cols,
        neighbor,
        single,
        ln_gain[None, :],
        w_hidden,
        b_hidden[None, :],
        w_mid,
        b_mid[None, :],
        w_logits.T,
        b_logits[:, None],
        R,
        C,
    )
    lddt_score, residue_loss, mean = finish(parts, logits, total, valid, R, C)
    return (lddt_score, residue_loss, mean[0, 0])


def solution(mesh):
    R = mesh.shape["row"]
    C = mesh.shape["col"]
    both = P(None, ("row", "col"))
    placed = (
        P(None, "col", "row"),
        P(None, None, ("row", "col")),
        P(None, None, ("row", "col")),
        both,
        P(None, ("row", "col"), None),
        P(),
        P(),
        P(),
        P(),
        P(),
        P(),
        P(),
    )
    return jax.shard_map(
        functools.partial(local, R, C),
        mesh=mesh,
        in_specs=placed,
        out_specs=(both, both, P()),
        check_vma=False,
    )
```

profile of v0, /device:TPU:0, one launch (start us, length us, event | category | flops | bytes accessed | tf_op | source)
XLA Modules:
  0.0 115.1 jit_solution(12334561213341659906)
XLA Ops:
  0.6 0.1 pad.3.clone
  0.7 1.2 %broadcast_in_dim.16.gain_ref = f32[1,384]{1,0:T(1,128)} reshape(f32[384]{0:T(512)} %param.17) | data formatting | bytes 3072 | tf_op jit(solution)/shard_map/broadcast_in_dim | solution.py:415
  1.9 0.7 convert_element_type.3.valid_ref
  2.6 0.0 copy-start
  2.6 1.4 %copy.18.bl_ref = f32[50,1]{1,0:T(8,128)} copy(f32[50,1]{0,1:T(1,128)} %bitcast.11) | data formatting | bytes 400 | tf_op jit(solution)/shard_map/broadcast_in_dim | solution.py:421
  4.0 0.8 copy.15
  4.8 0.8 copy.16
  5.7 0.7 maximum_maximum_fusion.x_ref
  6.4 26.2 %gather.1 = (f32[8,32,8,96]{3,2,1,0:T(8,128)}, f32[4,32,8,96]{3,2,1,0:T(8,128)}) custom-call(f32[32,8,96]{2,1,0:T(8,128)} %maximum_maximum_fusion.x_ref), custom_call_target="tpu_custom_call" | custom-call | tf_op jit(solution)/shard_map/gather/pallas_call | solution.py:104
  32.6 61.3 %pairs.1 = (f32[8,64,96]{2,1,0:T(8,128)}, f32[32,50,96]{2,1,0:T(8,128)}, f32[32,96]{1,0:T(8,128)}) custom-call(f32[8,32,8,96]{3,2,1,0:T(8,128)} %get-tuple-element.11.rows_ref, f32[4,32,8,96]{3,2,1,0:T(8,128)} %get-tuple-element.12.cols_ref, s32[32,384,768]{2,1,0:T(8,128)} %neighbor_ref.1, bf16[32,96,384]{2,1,0:T(8,128)(2,1)} %single_ref.1, ...), custom_call_target="tpu_custom_call" | custom-call | tf_op jit(solution)/shard_map/pairs/pallas_call | solution.py:234
  93.9 0.0 copy-done
  93.9 17.4 %finish.1 = (f32[32,96]{1,0:T(8,128)}, f32[32,96]{1,0:T(8,128)}, f32[8,128]{1,0:T(8,128)}) custom-call(f32[8,64,96]{2,1,0:T(8,128)} %get-tuple-element.13.parts_ref, f32[32,50,96]{2,1,0:T(8,128)} %get-tuple-element.14.logits_ref, f32[32,96]{1,0:T(8,128)} %get-tuple-element.15.total_ref, f32[32,96]{1,0:T(8,128)} %copy-done), custom_call_target="tpu_custom_call" | custom-call | tf_op jit(solution)/shard_map/finish/pallas_call | solution.py:363
  111.3 1.2 %slice.3 = f32[1,1]{1,0:T(1,128)} slice(f32[8,128]{1,0:T(8,128)} %get-tuple-element.18), slice={[0:1], [0:1]} | slice | bytes 8 | tf_op jit(solution)/shard_map/slice | solution.py:426
  112.5 1.3 %copy.21 = f32[32,96]{1,0:T(8,128)} copy(f32[32,96]{1,0:T(8,128)} %get-tuple-element.22) | data formatting | bytes 24576
  113.8 1.3 %copy.22 = f32[32,96]{1,0:T(8,128)} copy(f32[32,96]{1,0:T(8,128)} %get-tuple-element.23) | data formatting | bytes 24576
Async XLA Ops:
  2.6 91.3 %copy-start = (f32[32,96]{1,0:T(8,128)}, f32[32,96]{1,0:T(8,128)S(1)}, u32[]{:S(2)}) copy-start(f32[32,96]{1,0:T(8,128)S(1)} %convert_element_type.3.valid_ref) | copy-start | bytes 36868
where the time goes:
time: 116 us; the launch traced here: 115 us
  Pallas kernels  105 us (91%)
  local copies, waits for them, and re-layouts  8.16 us (7%)
  other arithmetic  1.44 us (1%)
    pallas_call x1, Pallas kernels, pairs(): pl.pallas_call(functools.partial(pair_kernel, R, C, 16), grid=(batch,), i...  61.3 us
    pallas_call x1, Pallas kernels, gather(): pl.pallas_call(functools.partial(gather_kernel, R, C), out_shape=(jax.Sha...  26.2 us
    pallas_call x1, Pallas kernels, finish(): pl.pallas_call(functools.partial(finish_kernel, R, C), out_shape=(jax.Sha...  17.4 us
    unnamed x6, local copies, waits for them, and re-layouts  4.32 us

commit v1 on v0

v1 whole, which is shorter than its diff:
```python
import functools

import jax
import jax.numpy as jnp
from jax import lax
from jax.experimental import pallas as pl
from jax.experimental.pallas import tpu as pltpu
from jax.sharding import PartitionSpec as P

THRESHOLDS = (0.5, 1.0, 2.0, 4.0)
EPS = 1e-10
MESH = pl.DeviceIdType.MESH
CHUNK = 4
WIDTH = 256
F32 = jnp.float32
BF16 = jnp.bfloat16


def split3(x):
    first = x.astype(BF16).astype(F32)
    rest = x - first
    second = rest.astype(BF16).astype(F32)
    return first, second, rest - second


def with_norms(x, row):
    square = x * x
    true_norm = square[0:1] + square[1:2] + square[2:3]
    pred_norm = square[3:4] + square[4:5] + square[5:6]
    mixed = jnp.where(row < 6, x, jnp.where(row == 6, true_norm, pred_norm))
    return mixed, true_norm, pred_norm


def build_sides(rows, cols, left_t, left_p, right):
    keep = cols[6:7]
    center = jnp.sum(cols * keep, axis=1, keepdims=True) / jnp.maximum(jnp.sum(keep, axis=1, keepdims=True), 1.0)
    row_r = lax.broadcasted_iota(jnp.int32, rows.shape, 0)
    row_c = lax.broadcasted_iota(jnp.int32, cols.shape, 0)
    far, _, _ = with_norms((rows - center) * 2.0, row_r)
    near = (cols - center) * 2.0
    _, near_t, near_p = with_norms(near, row_c)
    f1, f2, f3 = split3(far)
    ones = jnp.ones_like(far)
    right[...] = jnp.concatenate([f1, f1, f1, f2, f2, f3, ones, jnp.zeros_like(far)], axis=0).astype(BF16)
    n1, n2, n3 = split3(near)
    zeros = jnp.zeros_like(near)
    for ref, low, norm_row, norm in ((left_t, 0, 6, near_t), (left_p, 3, 7, near_p)):
        inside = (row_c >= low) & (row_c < low + 3)
        l1 = jnp.where(inside, -2.0 * n1, jnp.where(row_c == norm_row, 1.0, 0.0))
        l2 = jnp.where(inside, -2.0 * n2, 0.0)
        l3 = jnp.where(inside, -2.0 * n3, 0.0)
        m1, m2, m3 = split3(norm)
        tail = jnp.where(
            row_c == 0, m1, jnp.where(row_c == 1, m2, jnp.where(row_c == 2, m3, jnp.where(row_c == 3, 4.0 * EPS, 0.0)))
        )
        side = jnp.concatenate([l1, l2, l3, l1, l2, l1, tail, zeros], axis=0)
        ref[...] = jnp.transpose(side).astype(BF16)


def build_keep(cols, keep):
    count = jnp.sum(cols[6:7], axis=1, keepdims=True)
    index = lax.broadcasted_iota(jnp.int32, keep.shape, 0).astype(F32)
    keep[...] = jnp.where(index < count, 1.0, 0.0).astype(BF16)


def distances(left_t, left_p, right, d_true, d_pred, q):
    side = right[:, q * WIDTH : (q + 1) * WIDTH]
    d_true[q] = jnp.dot(left_t[...], side, preferred_element_type=F32)
    d_pred[q] = jnp.dot(left_p[...], side, preferred_element_type=F32)


def gaps(d_true, d_pred, floor, gap, q, j, h):
    span, lanes = slice(j, j + 16), slice(h * 128, h * 128 + 128)
    t2 = jnp.maximum(d_true[q, span, lanes], floor)
    p2 = jnp.maximum(d_pred[q, span, lanes], floor)
    gap[q, span, lanes] = jnp.abs(p2 * lax.rsqrt(p2) - t2 * lax.rsqrt(t2))


def scores(gap, neighbor_ref, keep, q, j, h, sums):
    span, lanes = slice(j, j + 16), slice(h * 128, h * 128 + 128)
    total, count = sums
    g = gap[q, span, lanes]
    at = slice(q * WIDTH + h * 128, q * WIDTH + h * 128 + 128)
    linked = neighbor_ref[0, span, at].astype(jnp.int16) != 0
    w = jnp.where(linked, keep[span, :], jnp.zeros((16, 128), BF16)).astype(F32)
    x2 = (2.0 * THRESHOLDS[1] - g).astype(BF16)
    for x in (
        (2.0 * THRESHOLDS[3] - g).astype(BF16),
        (2.0 * THRESHOLDS[2] - g).astype(BF16),
        x2,
        x2 - BF16(2.0 * (THRESHOLDS[1] - THRESHOLDS[0])),
    ):
        term = jnp.tanh(x).astype(F32) * w
        total = term if total is None else total + term
    one = w * w
    count = one if count is None else count + one
    return total, count


def head(b, single, gain, wh, bh, wm, bm, wl, bl, logits_ref, total_ref):
    features = single[b].astype(F32)
    average = jnp.mean(features, axis=-1, keepdims=True)
    centred = features - average
    variance = jnp.mean(centred * centred, axis=-1, keepdims=True)
    normed = (centred * lax.rsqrt(variance + 1e-05) * gain).astype(BF16)
    first = jnp.maximum(jnp.dot(normed, wh[...], preferred_element_type=F32) + bh[...], 0.0).astype(BF16)
    second = jnp.maximum(jnp.dot(first, wm[...], preferred_element_type=F32) + bm[...], 0.0).astype(BF16)
    logits = lax.dot_general(wl[...], second, (((1,), (1,)), ((), ())), preferred_element_type=F32) + bl
    logits_ref[b] = logits
    total_ref[pl.ds(b, 1), :] = jnp.log(jnp.sum(jnp.exp(logits), axis=0, keepdims=True))


def kernel(
    R, C,
    true_ref, pred_ref, mask_ref, neighbor_ref, single_ref, gain_ref, wh_ref, bh_ref, wm_ref, bm_ref, wl_ref, bl_ref,
    lddt_ref, loss_ref, mean_ref,
    x_ref, rows_ref, cols_ref, single_v, logits_ref, total_ref,
    left_t, left_p, right, keep, floor_ref, d_true, d_pred, gap, acc,
    parts, landed, tile, tiles,
    single_sem, send_sem, recv_sem, csend_sem, crecv_sem, psend_sem, precv_sem, tsend_sem, trecv_sem,
):
    b = pl.program_id(0)
    batch = pl.num_programs(0)
    count_b = x_ref.shape[0]
    own_len = mask_ref.shape[1]
    rows_len = C * own_len
    cols_len = R * own_len
    chunks = count_b // CHUNK
    r = lax.axis_index("row")
    c = lax.axis_index("col")
    g = r * C + c
    to_col = g // R
    slot = g % R
    own = to_col == c

    def part(ref, n):
        return ref.at[pl.ds(n * CHUNK, CHUNK)]

    def row_copy(k, n):
        return pltpu.make_async_remote_copy(
            src_ref=part(x_ref, n),
            dst_ref=part(rows_ref.at[c], n),
            send_sem=send_sem.at[k, n],
            recv_sem=recv_sem.at[k, n],
            device_id=(r, (c + k) % C),
            device_id_type=MESH,
        )

    def col_copy(k, n):
        return pltpu.make_async_remote_copy(
            src_ref=part(x_ref, n),
            dst_ref=part(cols_ref.at[slot], n),
            send_sem=csend_sem.at[k, n],
            recv_sem=crecv_sem.at[slot, n],
            device_id=((r + k) % R, to_col),
            device_id_type=MESH,
        )

    def col_arrival(s, n):
        return pltpu.make_async_remote_copy(
            src_ref=part(x_ref, n),
            dst_ref=part(cols_ref.at[s], n),
            send_sem=csend_sem.at[0, n],
            recv_sem=crecv_sem.at[s, n],
            device_id=(r, to_col),
            device_id_type=MESH,
        )

    def arrive(n):
        for k in range(1, C):
            row_copy(k, n).wait_recv()
        for s in range(R):

            @pl.when(R * c + s != g)
            def _():
                col_arrival(s, n).wait_recv()

    def all_rows(i):
        return jnp.concatenate([rows_ref[s, i] for s in range(C)], axis=1)

    def all_cols(i):
        return jnp.concatenate([cols_ref[s, i] for s in range(R)], axis=1)

    @pl.when(b == 0)
    def _():
        fetch = pltpu.make_async_copy(single_ref, single_v, single_sem)
        fetch.start()
        barrier = pltpu.get_barrier_semaphore()
        for k in range(1, R * C):
            other = (g + k) % (R * C)
            pl.semaphore_signal(barrier, inc=1, device_id=(other // C, other % C), device_id_type=MESH)
        for k in range(3):
            x_ref[:, k, :] = true_ref[k]
            x_ref[:, 3 + k, :] = pred_ref[k]
        x_ref[:, 6, :] = mask_ref[...].astype(F32)
        x_ref[:, 7, :] = jnp.zeros(mask_ref.shape, F32)
        floor_ref[...] = jnp.full(floor_ref.shape, 4.0 * EPS, F32)
        pl.semaphore_wait(barrier, R * C - 1)

        def send(n, carry):
            for k in range(1, R):
                col_copy(k, n).start()

            @pl.when(jnp.logical_not(own))
            def _():
                col_copy(0, n).start()

            for k in range(1, C):
                row_copy(k, n).start()
            return carry

        lax.fori_loop(0, chunks, send, 0)
        rows_ref[c] = x_ref[...]

        @pl.when(own)
        def _():
            cols_ref[slot] = x_ref[...]

        bins = wl_ref.shape[0]
        eye = lax.broadcasted_iota(jnp.int32, (bins, bins), 0) == lax.broadcasted_iota(jnp.int32, (bins, bins), 1)
        bl = jnp.sum(jnp.where(eye, bl_ref[...], 0.0), axis=1, keepdims=True)
        gain = gain_ref[...]
        fetch.wait()

        def heads(n, carry):
            for k in range(CHUNK):
                head(
                    n * CHUNK + k, single_v, gain, wh_ref, bh_ref, wm_ref, bm_ref, wl_ref, bl, logits_ref, total_ref
                )
            return carry

        lax.fori_loop(0, chunks, heads, 0)
        arrive(0)
        for i in range(2):
            build_sides(all_rows(i), all_cols(i), left_t, left_p, right)
            for q in range(rows_len // WIDTH):
                distances(left_t, left_p, right, d_true, d_pred, q)
                if i == 0:
                    for j in range(0, cols_len, 16):
                        for h in range(WIDTH // 128):
                            gaps(d_true, d_pred, floor_ref[...], gap, q, j, h)
        build_sides(all_rows(2), all_cols(2), left_t, left_p, right)
        build_keep(all_cols(0), keep)

    ahead = b + 3

    @pl.when((ahead % CHUNK == 0) & (ahead < batch))
    def _():
        arrive(ahead // CHUNK)

    floor = floor_ref[...]
    for q in range(rows_len // WIDTH):
        sums = [(None, None)] * (WIDTH // 128)
        for j in range(0, cols_len, 16):
            for h in range(WIDTH // 128):
                sums[h] = scores(gap, neighbor_ref, keep, q, j, h, sums[h])
                gaps(d_true, d_pred, floor, gap, q, j, h)
        distances(left_t, left_p, right, d_true, d_pred, q)
        for h in range(WIDTH // 128):
            at = slice(q * WIDTH + h * 128, q * WIDTH + h * 128 + 128)
            count = jnp.sum(sums[h][1], axis=0, keepdims=True)
            acc[b, 1:2, at] = count
            acc[b, 0:1, at] = 0.5 * count + 0.125 * jnp.sum(sums[h][0], axis=0, keepdims=True)
    later = jnp.minimum(ahead, batch - 1)
    build_sides(all_rows(later), all_cols(later), left_t, left_p, right)
    build_keep(all_cols(jnp.minimum(b + 1, batch - 1)), keep)

    @pl.when(b == batch - 1)
    def _():
        for s in range(C):
            lanes = slice(s * own_len, (s + 1) * own_len)
            parts[s, 0:count_b, :] = acc[:, 0, lanes]
            parts[s, count_b:, :] = acc[:, 1, lanes]
        copies = []
        for k in range(1, C):
            peer = (c + k) % C
            copy = pltpu.make_async_remote_copy(
                src_ref=parts.at[peer],
                dst_ref=landed.at[k],
                send_sem=psend_sem.at[k],
                recv_sem=precv_sem.at[k],
                device_id=(r, peer),
                device_id_type=MESH,
            )
            copy.start()
            copies.append(copy)
        sums = parts[c]

        def sent(n, carry):
            for k in range(1, R):
                col_copy(k, n).wait_send()

            @pl.when(jnp.logical_not(own))
            def _():
                col_copy(0, n).wait_send()

            for k in range(1, C):
                row_copy(k, n).wait_send()
            return carry

        lax.fori_loop(0, chunks, sent, 0)
        for copy in copies:
            copy.wait()
        for k in range(1, C):
            sums = sums + landed[k]
        valid = x_ref[:, 6, :]
        lddt = valid * sums[0:count_b] / jnp.maximum(valid * sums[count_b:], 1.0)
        lddt_ref[...] = lddt
        bins = logits_ref.shape[1]
        logits = logits_ref[...]
        centers = (lax.broadcasted_iota(jnp.int32, logits.shape, 1).astype(F32) + 0.5) / bins
        apart = lddt[:, None, :] - centers
        closeness = jnp.exp(-(apart * apart) * (bins * bins * 0.5))
        expected = jnp.sum(closeness * logits, axis=1) / jnp.sum(closeness, axis=1)
        loss = valid * (total_ref[...] - expected)
        tile[...] = jnp.zeros_like(tile)
        tile[0:1, 0:own_len] = jnp.sum(loss, axis=0, keepdims=True)
        tile[1:2, 0:own_len] = jnp.sum(valid, axis=0, keepdims=True)
        loss_ref[...] = loss
        copies = []
        for k in range(1, R * C):
            other = (g + k) % (R * C)
            copy = pltpu.make_async_remote_copy(
                src_ref=tile,
                dst_ref=tiles.at[g],
                send_sem=tsend_sem.at[k],
                recv_sem=trecv_sem.at[k],
                device_id=(other // C, other % C),
                device_id_type=MESH,
            )
            copy.start()
            copies.append(copy)
        tiles[g] = tile[...]
        for copy in copies:
            copy.wait()
        final = tiles[0]
        for k in range(1, R * C):
            final = final + tiles[k]
        both = jnp.sum(final, axis=1, keepdims=True)
        mean_ref[...] = jnp.broadcast_to(both[0:1] / both[1:2], mean_ref.shape)


def local(
    R, C,
    neighbor,
    true_coords,
    pred_coords,
    residue_mask,
    single,
    ln_gain,
    w_hidden,
    b_hidden,
    w_mid,
    b_mid,
    w_logits,
    b_logits,
):
    batch, own_len = residue_mask.shape
    cols_len, rows_len = neighbor.shape[1:]
    bins = w_logits.shape[1]
    whole = pl.BlockSpec(memory_space=pltpu.VMEM)
    chunks = batch // CHUNK
    tiles = rows_len // WIDTH
    dma = pltpu.SemaphoreType.DMA
    lddt, loss, mean = pl.pallas_call(
        functools.partial(kernel, R, C),
        grid=(batch,),
        in_specs=[
            whole,
            whole,
            whole,
            pl.BlockSpec((1, cols_len, rows_len), lambda i: (i, 0, 0)),
            pl.BlockSpec(memory_space=pl.ANY),
        ]
        + [whole] * 7,
        out_specs=[whole] * 3,
        out_shape=[
            jax.ShapeDtypeStruct((batch, own_len), F32),
            jax.ShapeDtypeStruct((batch, own_len), F32),
            jax.ShapeDtypeStruct((8, 128), F32),
        ],
        scratch_shapes=[
            pltpu.VMEM((batch, 8, own_len), F32),
            pltpu.VMEM((C, batch, 8, own_len), F32),
            pltpu.VMEM((R, batch, 8, own_len), F32),
            pltpu.VMEM(single.shape, single.dtype),
            pltpu.VMEM((batch, bins, own_len), F32),
            pltpu.VMEM((batch, own_len), F32),
            pltpu.VMEM((cols_len, 64), BF16),
            pltpu.VMEM((cols_len, 64), BF16),
            pltpu.VMEM((64, rows_len), BF16),
            pltpu.VMEM((cols_len, 128), BF16),
            pltpu.VMEM((16, 128), F32),
            pltpu.VMEM((tiles, cols_len, WIDTH), F32),
            pltpu.VMEM((tiles, cols_len, WIDTH), F32),
            pltpu.VMEM((tiles, cols_len, WIDTH), F32),
            pltpu.VMEM((batch, 2, rows_len), F32),
            pltpu.VMEM((C, 2 * batch, own_len), F32),
            pltpu.VMEM((C, 2 * batch, own_len), F32),
            pltpu.VMEM((8, 128), F32),
            pltpu.VMEM((R * C, 8, 128), F32),
            dma,
            dma((C, chunks)),
            dma((C, chunks)),
            dma((R, chunks)),
            dma((R, chunks)),
            dma((C,)),
            dma((C,)),
            dma((R * C,)),
            dma((R * C,)),
        ],
        compiler_params=pltpu.CompilerParams(
            dimension_semantics=("arbitrary",), collective_id=0, has_side_effects=True
        ),
        name="lddt",
    )(
        jnp.transpose(true_coords, (1, 0, 2)),
        jnp.transpose(pred_coords, (1, 0, 2)),
        residue_mask,
        neighbor,
        single,
        ln_gain[None, :],
        w_hidden,
        b_hidden[None, :],
        w_mid,
        b_mid[None, :],
        w_logits.T,
        b_logits[None, :],
    )
    return (lddt, loss, mean[0, 0])


def solution(mesh):
    R = mesh.shape["row"]
    C = mesh.shape["col"]
    both = P(None, ("row", "col"))
    placed = (
        P(None, "col", "row"),
        P(None, None, ("row", "col")),
        P(None, None, ("row", "col")),
        both,
        P(None, ("row", "col"), None),
        P(),
        P(),
        P(),
        P(),
        P(),
        P(),
        P(),
    )
    return jax.shard_map(
        functools.partial(local, R, C),
        mesh=mesh,
        in_specs=placed,
        out_specs=(both, both, P()),
        check_vma=False,
    )
```

time: 116 us -> 83 us (0.72)
  Pallas kernels: 105 us -> 76.4 us
  local copies, waits for them, and re-layouts: 8.16 us -> 5.08 us
  other arithmetic: 1.44 us -> 0 us
    pallas_call x3 -> x1, Pallas kernels: 105 us -> 76.4 us  [local(): pl.pallas_call(functools.partial(kernel, R, C), grid=(batch,), in_specs=[...]
    unnamed x6 -> x2, local copies, waits for them, and re-layouts: 4.32 us -> 2.65 us
    broadcast_in_dim x1 -> x0, local copies, waits for them, and re-layouts: 1.35 us -> none  [local(): b_logits[:, None]]
where the time goes in v1:
time: 83 us; the launch traced here: 82.1 us
  Pallas kernels  76.4 us (92%)
  local copies, waits for them, and re-layouts  5.08 us (6%)
    pallas_call x1, Pallas kernels, local(): pl.pallas_call(functools.partial(kernel, R, C), grid=(batch,), in_specs=[...  76.4 us
    unnamed x2, local copies, waits for them, and re-layouts  2.65 us

profile of v1, /device:TPU:0, one launch (start us, length us, event | category | flops | bytes accessed | tf_op | source)
XLA Modules:
  0.0 82.1 jit_solution(9104036460879237897)
XLA Ops:
  0.6 1.2 %broadcast_in_dim.12.gain_ref = f32[1,384]{1,0:T(1,128)} reshape(f32[384]{0:T(512)} %param.17) | data formatting | bytes 3072 | tf_op jit(solution)/shard_map/broadcast_in_dim | solution.py:422
  1.9 76.4 %lddt.1 = (f32[32,96]{1,0:T(8,128)}, f32[32,96]{1,0:T(8,128)}, f32[8,128]{1,0:T(8,128)}) custom-call(f32[3,32,96]{2,1,0:T(8,128)} %bitcast.7, f32[3,32,96]{2,1,0:T(8,128)} %bitcast.8, s32[32,96]{1,0:T(8,128)} %mask_ref.1, s32[32,384,768]{2,1,0:T(8,128)} %neighbor_ref.1, bf16[32,96,384]{2,1,0:T(8,128)(2,1)} %single_ref.1, ...), custom_call_target="tpu_custom_call" | custom-call | tf_op jit(solution)/shard_map/lddt/pallas_call | solution.py:365
  78.3 1.2 %slice.3 = f32[1,1]{1,0:T(1,128)} slice(f32[8,128]{1,0:T(8,128)} %get-tuple-element.8), slice={[0:1], [0:1]} | slice | bytes 8 | tf_op jit(solution)/shard_map/slice | solution.py:430
  79.5 1.3 %copy.17 = f32[32,96]{1,0:T(8,128)} copy(f32[32,96]{1,0:T(8,128)} %get-tuple-element.12) | data formatting | bytes 24576
  80.8 1.3 %copy.18 = f32[32,96]{1,0:T(8,128)} copy(f32[32,96]{1,0:T(8,128)} %get-tuple-element.13) | data formatting | bytes 24576
